TPU v7x, 32 devices: a whole 2x2x4 slice. The times are simulated.
32 devices in a mesh: expert: 16 (over z, y, core), dp: 2 (over x).
Axes of the slice: x: 2, y: 2, z: 4, core: 2. Of those that a mesh axis runs over, the one named last changes fastest.
Arguments:
- tokens: bfloat16 [4096, 2880], P(('expert', 'dp')), may hold values from -6 to 6
- cotangent: bfloat16 [4096, 2880], P(('expert', 'dp')), may hold values from -3 to 3
- expert_ids: int32 [4096, 4], P(('expert', 'dp')), may hold values from 0 to 15, as said below
- slots: int32 [4096, 4], P(('expert', 'dp')), may hold values from -1 to 23, as said below
- probs: float32 [4096, 4], P(('expert', 'dp')), may hold values from 0.1 to 0.6
- w_gate: bfloat16 [16, 2880, 1440], P('expert', None, 'dp'), may hold values from -0.109375 to 0.109375
- w_up: bfloat16 [16, 2880, 1440], P('expert', None, 'dp'), may hold values from -0.109375 to 0.109375
- w_down: bfloat16 [16, 2880, 1440], P('expert', None, 'dp'), may hold values from -0.15625 to 0.15625
Outputs:
- input_grad: bfloat16 [4096, 2880], P(('expert', 'dp'))
- prob_grad: float32 [4096, 4], P(('expert', 'dp'))
- grad_gate: bfloat16 [16, 2880, 1440], P('expert', None, 'dp')
- grad_up: bfloat16 [16, 2880, 1440], P('expert', None, 'dp')
- grad_down: bfloat16 [16, 2880, 1440], P('expert', None, 'dp')
Inputs may be any that keep to these rules, and one draw needn't show every extreme that they name: `expert_ids`: each row names 4 different experts. Within the 128 tokens of one device, the choices of one expert, taken in order of tokens and then of k, hold 0, 1, 2 and so on up to 23, and -1 after that; in every draw some expert fills all 24 slots from every device.
All inputs are finite; a program needn't handle non-finite values.
Results may differ from a plain program's by a relative error of at most 0.018.
Values may be sent and summed in bfloat16 or wider, within the bound.
A program may use at most 192 MiB of HBM per device.

v0:
```python
import jax
import jax.numpy as jnp
from jax import lax
from jax.sharding import PartitionSpec as P

ALPHA = 1.702


def body(tokens, cotangent, expert_ids, slots, probs, w_gate, w_up, w_down):
    experts = lax.axis_size("expert")
    tok_rows = tokens.shape[0]
    width = tokens.shape[1]
    top_count = expert_ids.shape[1]
    capacity = max(2, 3 * tok_rows * top_count // (4 * experts))
    slot_total = experts * capacity
    kept = slots >= 0
    position = jnp.where(kept, expert_ids * capacity + slots, slot_total)
    owners = jnp.broadcast_to(jnp.arange(tok_rows, dtype=jnp.int32)[:, None], expert_ids.shape)
    slot_owner = (
        jnp.full((slot_total,), -1, jnp.int32)
        .at[position.reshape(-1)]
        .set(owners.reshape(-1), mode="drop")
    )
    slot_prob = (
        jnp.zeros((slot_total,), jnp.float32)
        .at[position.reshape(-1)]
        .set(probs.reshape(-1), mode="drop")
    )
    present = slot_owner >= 0
    source = jnp.maximum(slot_owner, 0)
    lookup = jnp.where(kept, expert_ids * capacity + slots, 0)
    zero_bf = jnp.zeros((), jnp.bfloat16)
    outgoing = jnp.where(present[:, None], tokens[source], zero_bf)
    arrived = lax.all_to_all(
        outgoing.reshape(experts, capacity, width),
        "expert",
        split_axis=0,
        concat_axis=0,
        tiled=True,
    )
    local_rows = arrived.reshape(slot_total, width)
    pair_rows = lax.all_gather(local_rows, "dp", axis=0, tiled=True)
    gate_w = w_gate[0]
    up_w = w_up[0]
    down_w = w_down[0]
    gate_pre = jnp.dot(pair_rows, gate_w, preferred_element_type=jnp.float32)
    up_pre = jnp.dot(pair_rows, up_w, preferred_element_type=jnp.float32)
    sigmoid_val = jax.nn.sigmoid(ALPHA * gate_pre)
    glu_value = gate_pre * sigmoid_val
    hidden = ((up_pre + 1.0) * glu_value).astype(jnp.bfloat16)
    contract_units = (((1,), (1,)), ((), ()))
    contract_rows = (((0,), (0,)), ((), ()))
    own_out = lax.psum_scatter(
        lax.dot_general(hidden, down_w, contract_units, preferred_element_type=jnp.float32).astype(
            jnp.bfloat16
        ),
        "dp",
        scatter_dimension=0,
        tiled=True,
    )
    returned = lax.all_to_all(
        own_out.reshape(experts, capacity, width), "expert", split_axis=0, concat_axis=0, tiled=True
    )
    picked_out = returned.reshape(slot_total, width)[lookup]
    inner = jnp.einsum("tkd,td->tk", picked_out, cotangent, preferred_element_type=jnp.float32)
    prob_grad = jnp.where(kept, inner, jnp.float32(0.0))
    weighted_send = jnp.where(
        present[:, None],
        (slot_prob[:, None] * cotangent[source].astype(jnp.float32)).astype(jnp.bfloat16),
        zero_bf,
    )
    weighted = lax.all_to_all(
        weighted_send.reshape(experts, capacity, width),
        "expert",
        split_axis=0,
        concat_axis=0,
        tiled=True,
    )
    weighted = weighted.reshape(slot_total, width)
    pair_cot = lax.all_gather(weighted, "dp", axis=0, tiled=True)
    hidden_grad = jnp.dot(pair_cot, down_w, preferred_element_type=jnp.float32)
    up_grad = (hidden_grad * glu_value).astype(jnp.bfloat16)
    gate_grad = (
        hidden_grad
        * (up_pre + 1.0)
        * (sigmoid_val + ALPHA * gate_pre * sigmoid_val * (1.0 - sigmoid_val))
    ).astype(jnp.bfloat16)
    grad_down = lax.dot_general(
        pair_cot, hidden, contract_rows, preferred_element_type=jnp.float32
    ).astype(jnp.bfloat16)
    grad_gate = lax.dot_general(
        pair_rows, gate_grad, contract_rows, preferred_element_type=jnp.float32
    ).astype(jnp.bfloat16)
    grad_up = lax.dot_general(
        pair_rows, up_grad, contract_rows, preferred_element_type=jnp.float32
    ).astype(jnp.bfloat16)
    result = lax.dot_general(gate_grad, gate_w, contract_units, preferred_element_type=jnp.float32)
    own_input = lax.psum_scatter(
        (
            result
            + lax.dot_general(up_grad, up_w, contract_units, preferred_element_type=jnp.float32)
        ).astype(jnp.bfloat16),
        "dp",
        scatter_dimension=0,
        tiled=True,
    )
    back_rows = lax.all_to_all(
        own_input.reshape(experts, capacity, width),
        "expert",
        split_axis=0,
        concat_axis=0,
        tiled=True,
    )
    back_rows = back_rows.reshape(slot_total, width)
    picked_grad = back_rows[lookup]
    masked = jnp.where(kept[:, :, None], picked_grad, zero_bf)
    input_grad = jnp.sum(masked, axis=1, dtype=jnp.float32).astype(jnp.bfloat16)
    return (input_grad, prob_grad, grad_gate[None], grad_up[None], grad_down[None])


def solution(mesh):
    return jax.shard_map(
        body,
        mesh=mesh,
        in_specs=(
            P(("expert", "dp"), None),
            P(("expert", "dp"), None),
            P(("expert", "dp"), None),
            P(("expert", "dp"), None),
            P(("expert", "dp"), None),
            P("expert", None, "dp"),
            P("expert", None, "dp"),
            P("expert", None, "dp"),
        ),
        out_specs=(
            P(("expert", "dp"), None),
            P(("expert", "dp"), None),
            P("expert", None, "dp"),
            P("expert", None, "dp"),
            P("expert", None, "dp"),
        ),
        check_vma=False,
    )
```

profile of v0, /device:TPU:13, one launch (start us, length us, event | category | flops | bytes accessed | tf_op | source)
XLA Modules:
  0.0 436.5 jit_solution(271618593306494350)
XLA Ops:
  24.1 3.9 broadcast_select_fusion
  28.1 57.2 %all_to_all.20 = bf16[16,24,2880]{2,1,0:T(8,128)(2,1)} all-to-all(bf16[16,24,2880]{2,1,0:T(8,128)(2,1)S(1)} %get-tuple-element.15), channel_id=1, replica_groups=mesh['expert'=16,'dp'=2] {'expert'}, dimensions={0} | all-to-all | bytes 4423680 | tf_op jit(solution)/shard_map/all_to_all | solution.py:34
  85.3 56.1 %all_to_all.21 = bf16[16,24,2880]{2,1,0:T(8,128)(2,1)} all-to-all(bf16[16,24,2880]{2,1,0:T(8,128)(2,1)S(1)} %get-tuple-element.16), channel_id=1, replica_groups=mesh['expert'=16,'dp'=2] {'expert'}, dimensions={0} | all-to-all | bytes 4423680 | tf_op jit(solution)/shard_map/all_to_all | solution.py:72
  145.4 6.8 %fusion.6 = f32[768,720]{0,1:T(8,128)S(1)} fusion(bf16[768,2880]{1,0:T(8,128)(2,1)} %all-gather.5.cloned.1.call-done, bf16[1,2880,720]{1,2,0:T(8,128)(2,1)} %param.13), kind=kOutput, calls=%fused_computation.19 | convolution fusion | flops 3185049600 | bytes 10782720 | tf_op jit(solution)/shard_map/dot_general | solution.py:46
  152.2 55.2 %all-gather.3.cloned.1.call-done = bf16[768,2880]{1,0:T(8,128)(2,1)} async-done(((bf16[384,2880]{1,0:T(8,128)(2,1)}), bf16[768,2880]{1,0:T(8,128)(2,1)}) %all-gather.3.cloned.1.call-update) | async-done | bytes 4423696 | tf_op jit(solution)/shard_map/all_gather | solution.py:80
  207.4 6.9 %fusion.12 = f32[768,720]{0,1:T(8,128)S(1)} fusion(bf16[768,2880]{1,0:T(8,128)(2,1)} %all-gather.3.cloned.1.call-done, bf16[1,2880,720]{1,2,0:T(8,128)(2,1)} %param.15), kind=kOutput, calls=%fused_computation.25 | convolution fusion | flops 3185049600 | bytes 10782720 | tf_op jit(solution)/shard_map/dot_general | solution.py:81
  214.4 7.7 %multiply_convert_fusion = (bf16[768,720]{0,1:T(8,128)(2,1)}, bf16[768,720]{0,1:T(8,128)(2,1)S(1)}, bf16[768,720]{0,1:T(8,128)(2,1)S(1)}) fusion(f32[768,720]{0,1:T(8,128)S(1)} %fusion.6, f32[768,720]{0,1:T(8,128)S(1)} %fusion.12, bf16[768,2880]{1,0:T(8,128)(2,1)S(1)} %copy-done.2, bf16[1,2880,720]{1,2,0:T(8,128)(2,1)} %param.14), kind=kOutput, calls=%fused_computation.30 | convolution fusion | flops 3194449920 | bytes 16312320 | tf_op jit(solution)/shard_map/dot_general | solution.py:47
  222.1 4.0 fusion.4
  226.2 5.9 %add_convert_fusion = bf16[768,2880]{0,1:T(8,128)(2,1)} fusion(f32[768,2880]{0,1:T(8,128)S(1)} %fusion.4, bf16[768,720]{0,1:T(8,128)(2,1)S(1)} %get-tuple-element.14, bf16[1,2880,720]{1,2,0:T(8,128)(2,1)S(1)} %bitcast.63), kind=kOutput, calls=%fused_computation.6 | convolution fusion | flops 3189473280 | bytes 18524160 | tf_op jit(solution)/shard_map/dot_general | solution.py:101
  232.1 6.6 %copy.40 = bf16[768,2880]{1,0:T(8,128)(2,1)} copy(bf16[768,2880]{0,1:T(8,128)(2,1)} %add_convert_fusion) | data formatting | bytes 8847360
  239.9 8.0 %convolution_convert_fusion = bf16[768,2880]{0,1:T(8,128)(2,1)} fusion(bf16[768,720]{0,1:T(8,128)(2,1)S(1)} %copy-done.6, bf16[1,2880,720]{1,2,0:T(8,128)(2,1)} %param.15), kind=kOutput, calls=%fused_computation.8 | convolution fusion | flops 3187261440 | bytes 9676800 | tf_op jit(solution)/shard_map/dot_general | solution.py:54
  247.9 6.5 %copy.42 = bf16[768,2880]{1,0:T(8,128)(2,1)} copy(bf16[768,2880]{0,1:T(8,128)(2,1)} %convolution_convert_fusion) | data formatting | bytes 8847360
  254.5 42.3 %reduce-scatter.7.cloned.1.call-done = bf16[384,2880]{1,0:T(8,128)(2,1)} async-done(((bf16[768,2880]{1,0:T(8,128)(2,1)}), bf16[384,2880]{1,0:T(8,128)(2,1)}) %reduce-scatter.7.cloned.1.call-update) | async-done | bytes 2211856 | tf_op jit(solution)/shard_map/reduce_scatter | solution.py:98
  296.8 6.5 %all-to-all-start.2 = ((bf16[16,24,2880]{2,1,0:T(8,128)(2,1)}), bf16[16,24,2880]{2,1,0:T(8,128)(2,1)S(1)}, u32[]{:S(2)}, u32[]{:S(2)}) async-start(bf16[16,24,2880]{2,1,0:T(8,128)(2,1)} %bitcast.55), calls=%async_computation.2 | async-start | bytes 4521984 | tf_op jit(solution)/shard_map/all_to_all | solution.py:107
  303.3 53.6 %reduce-scatter.9.cloned.1.call-done = bf16[384,2880]{1,0:T(8,128)(2,1)} async-done(((bf16[768,2880]{1,0:T(8,128)(2,1)}), bf16[384,2880]{1,0:T(8,128)(2,1)}) %reduce-scatter.9.cloned.1.call-update) | async-done | bytes 2211856 | tf_op jit(solution)/shard_map/reduce_scatter | solution.py:53
  356.9 6.5 %all-to-all-start.3 = ((bf16[16,24,2880]{2,1,0:T(8,128)(2,1)}), bf16[16,24,2880]{2,1,0:T(8,128)(2,1)}, u32[]{:S(2)}, u32[]{:S(2)}) async-start(bf16[16,24,2880]{2,1,0:T(8,128)(2,1)} %bitcast.54), calls=%async_computation.3 | async-start | bytes 4521984 | tf_op jit(solution)/shard_map/all_to_all | solution.py:61
  365.3 8.4 %fusion.1 = bf16[1,2880,720]{1,2,0:T(8,128)(2,1)} fusion(bf16[768,720]{0,1:T(8,128)(2,1)} %copy-done.5, bf16[768,2880]{1,0:T(8,128)(2,1)} %all-gather.5.cloned.1.call-done), kind=kOutput, calls=%fused_computation.14 | convolution fusion | flops 3187123200 | bytes 9676800 | tf_op jit(solution)/shard_map/dot_general | solution.py:91
  373.7 7.5 %fusion.2 = bf16[1,2880,720]{1,2,0:T(8,128)(2,1)} fusion(bf16[768,720]{0,1:T(8,128)(2,1)S(1)} %copy-done.4, bf16[768,2880]{1,0:T(8,128)(2,1)} %all-gather.5.cloned.1.call-done), kind=kOutput, calls=%fused_computation.15 | convolution fusion | flops 3187123200 | bytes 9676800 | tf_op jit(solution)/shard_map/dot_general | solution.py:94
  381.2 5.2 %fusion.3 = bf16[1,2880,720]{1,2,0:T(8,128)(2,1)} fusion(bf16[768,720]{0,1:T(8,128)(2,1)S(1)} %copy-done.7, bf16[768,2880]{1,0:T(8,128)(2,1)S(1)} %bitcast.59), kind=kOutput, calls=%fused_computation.16 | convolution fusion | flops 3187123200 | bytes 9676800 | tf_op jit(solution)/shard_map/dot_general | solution.py:88
  390.1 4.7 %reshape.116 = bf16[128,4,2880]{2,1,0:T(4,128)(2,1)S(1)} reshape(bf16[512,2880]{1,0:T(8,128)(2,1)} %gather_fusion.2) | data formatting | bytes 5898240 | tf_op jit(solution)/shard_map/gather | solution.py:115
  394.8 4.2 select_reduce_fusion
  401.2 13.2 %all-to-all-done.3 = bf16[16,24,2880]{2,1,0:T(8,128)(2,1)} async-done(((bf16[16,24,2880]{2,1,0:T(8,128)(2,1)}), bf16[16,24,2880]{2,1,0:T(8,128)(2,1)}, u32[]{:S(2)}, u32[]{:S(2)}) %all-to-all-start.3) | async-done | bytes 2211872 | tf_op jit(solution)/shard_map/all_to_all | solution.py:61
  414.5 8.0 %gather_fusion.3 = bf16[512,2880]{1,0:T(8,128)(2,1)S(1)} fusion(bf16[384,2880]{1,0:T(8,128)(2,1)} %bitcast.12, s32[1024]{0:T(1024)S(1)} %pad_clamp_fusion), kind=kCustom, calls=%fused_computation.3 | custom fusion | bytes 5900288 | tf_op jit(solution)/shard_map/gather | solution.py:64
  424.9 4.0 multiply_reduce_fusion
  (71 shorter events, 33.0 us)
Async XLA Ops:
  7.2 138.3 %all-gather.5.cloned.1.call-start = ((), (), s32[]{:S(2)}) async-start(), calls=%async_computation.7 | async-start | bytes 6782976 | tf_op jit(solution)/shard_map/all_gather | solution.py:42
  17.8 3.5 copy-start.1
  85.3 122.1 %all-gather.3.cloned.1.call-start = ((), (), s32[]{:S(2)}) async-start(), calls=%async_computation.6 | async-start | bytes 6782976 | tf_op jit(solution)/shard_map/all_gather | solution.py:80
  141.5 155.3 %reduce-scatter.7.cloned.1.call-start = ((), (), s32[]{:S(2)}) async-start(), calls=%async_computation.8 | async-start | bytes 6782976 | tf_op jit(solution)/shard_map/reduce_scatter | solution.py:98
  207.4 6.9 %copy-start.2 = (bf16[768,2880]{1,0:T(8,128)(2,1)S(1)}, bf16[768,2880]{1,0:T(8,128)(2,1)}, u32[]{:S(2)}) copy-start(bf16[768,2880]{1,0:T(8,128)(2,1)} %all-gather.5.cloned.1.call-done) | copy-start | bytes 13271044
  207.4 14.6 %slice-start.2 = ((s8[4239360]{0:T(1024)(128)(4,1)}), s8[4194304]{0:T(1024)(128)(4,1)S(1)}, s32[]{:S(2)}) async-start(s8[4239360]{0:T(1024)(128)(4,1)} %bitcast.60), calls=%async_computation.12 | async-start | bytes 8388608
  207.4 18.7 %slice-start.4 = ((s8[4239360]{0:T(1024)(128)(4,1)}), s8[4194304]{0:T(1024)(128)(4,1)S(1)}, s32[]{:S(2)}) async-start(s8[4239360]{0:T(1024)(128)(4,1)} %bitcast.62), calls=%async_computation.14 | async-start | bytes 8388608
  214.4 7.7 %slice-start.3 = ((s8[4239360]{0:T(1024)(128)(4,1)}), s8[45056]{0:T(1024)(128)(4,1)S(1)}, s32[]{:S(2)}) async-start(s8[4239360]{0:T(1024)(128)(4,1)} %bitcast.60), calls=%async_computation.13 | async-start | bytes 90112
  214.4 11.8 %slice-start.5 = ((s8[4239360]{0:T(1024)(128)(4,1)}), s8[45056]{0:T(1024)(128)(4,1)S(1)}, s32[]{:S(2)}) async-start(s8[4239360]{0:T(1024)(128)(4,1)} %bitcast.62), calls=%async_computation.15 | async-start | bytes 90112
  222.1 4.1 copy-start.5
  222.1 4.1 copy-start.3
  238.7 1.2 copy-start.6
  238.7 118.2 %reduce-scatter.9.cloned.1.call-start = ((), (), s32[]{:S(2)}) async-start(), calls=%async_computation.9 | async-start | bytes 6782976 | tf_op jit(solution)/shard_map/reduce_scatter | solution.py:53
  296.8 60.1 %all-to-all-start.2 = ((bf16[16,24,2880]{2,1,0:T(8,128)(2,1)}), bf16[16,24,2880]{2,1,0:T(8,128)(2,1)S(1)}, u32[]{:S(2)}, u32[]{:S(2)}) async-start(bf16[16,24,2880]{2,1,0:T(8,128)(2,1)} %bitcast.55), calls=%async_computation.2 | async-start | bytes 4521984 | tf_op jit(solution)/shard_map/all_to_all | solution.py:107
  303.3 60.3 %copy-start = (bf16[128,2880]{0,1:T(8,128)(2,1)S(1)}, bf16[128,2880]{0,1:T(8,128)(2,1)}, u32[]{:S(2)}) copy-start(bf16[128,2880]{0,1:T(8,128)(2,1)} %param.9) | copy-start | bytes 2211844
  356.9 57.5 %all-to-all-start.3 = ((bf16[16,24,2880]{2,1,0:T(8,128)(2,1)}), bf16[16,24,2880]{2,1,0:T(8,128)(2,1)}, u32[]{:S(2)}, u32[]{:S(2)}) async-start(bf16[16,24,2880]{2,1,0:T(8,128)(2,1)} %bitcast.54), calls=%async_computation.3 | async-start | bytes 4521984 | tf_op jit(solution)/shard_map/all_to_all | solution.py:61
  365.2 8.4 %copy-start.4 = (bf16[768,720]{0,1:T(8,128)(2,1)S(1)}, bf16[768,720]{0,1:T(8,128)(2,1)}, u32[]{:S(2)}) copy-start(bf16[768,720]{0,1:T(8,128)(2,1)} %copy-done.3) | copy-start | bytes 3317764
  365.3 15.9 %slice-start = ((s8[4521984]{0:T(1024)(128)(4,1)}), s8[4194304]{0:T(1024)(128)(4,1)S(1)}, s32[]{:S(2)}) async-start(s8[4521984]{0:T(1024)(128)(4,1)} %bitcast.58), calls=%async_computation.10 | async-start | bytes 8388608
  373.6 7.6 %slice-start.1 = ((s8[4521984]{0:T(1024)(128)(4,1)}), s8[327680]{0:T(1024)(128)(4,1)S(1)}, s32[]{:S(2)}) async-start(s8[4521984]{0:T(1024)(128)(4,1)} %bitcast.58), calls=%async_computation.11 | async-start | bytes 655360
  373.7 7.6 %copy-start.7 = (bf16[768,720]{0,1:T(8,128)(2,1)S(1)}, bf16[768,720]{0,1:T(8,128)(2,1)}, u32[]{:S(2)}) copy-start(bf16[768,720]{0,1:T(8,128)(2,1)} %get-tuple-element.12) | copy-start | bytes 3317764
Sparse Core Ops, SparseCore 0:
  85.4 59.9 all-gather.4
  147.0 60.4 all-gather.2
  238.8 57.9 reduce-scatter.6
  298.9 57.9 reduce-scatter.8
where the time goes:
time: 443 us; the launch traced here: 436 us
  waiting for transfers between devices  168 us (38%)
  blocking collectives  113 us (26%)
  matrix products  60.4 us (14%)
  local copies, waits for them, and re-layouts  52.4 us (12%)
  between operations  14.5 us (3%)
  other arithmetic  14.1 us (3%)
  starting transfers between devices  13.6 us (3%)
    all_to_all x1, blocking collectives, body(): lax.all_to_all(outgoing.reshape(experts, capacity, width), 'expert', spli...  57.2 us
    all_to_all x1, blocking collectives, body(): lax.all_to_all(weighted_send.reshape(experts, capacity, width), 'expert',...  56.1 us
    all_gather x1, waiting for transfers between devices, body(): pair_cot = lax.all_gather(weighted, 'dp', axis=0, tiled=True)  55.2 us
    reduce_scatter x1, waiting for transfers between devices, body(): lax.psum_scatter(lax.dot_general(hidden, down_w, contract_units, preferre...  53.6 us
    reduce_scatter x1, waiting for transfers between devices, body(): lax.psum_scatter((result + lax.dot_general(up_grad, up_w, contract_units,...  42.3 us
    unnamed x35, local copies, waits for them, and re-layouts  20.8 us
    all_to_all x1, waiting for transfers between devices, body(): lax.all_to_all(own_out.reshape(experts, capacity, width), 'expert', split...  13.2 us
    gather x2, local copies, waits for them, and re-layouts, body(): picked_out = returned.reshape(slot_total, width)[lookup]  10.4 us
  transfers between devices with their start and end apart: 6, of which 5 were waited for; matrix products, arithmetic and copies ran while one was open for 14% of the time, Pallas kernels for 0%

commit v1 on v0

v1 whole, which is shorter than its diff:
```python
import functools

import jax
import jax.numpy as jnp
from jax import lax
from jax.experimental import pallas as pl
from jax.experimental.pallas import tpu as pltpu
from jax.sharding import PartitionSpec as P

ALPHA = 1.702
MESH = pl.DeviceIdType.MESH
ANY = pl.BlockSpec(memory_space=pl.ANY)


def offsets_of(count):
    half = count // 2
    order = []
    for step in range(half):
        order.append(half + step)
        if step:
            order.append(step)
    return order


def dispatch_kernel(count, tok_ref, cot_ref, rows_ref, wrows_ref, local_sem, send_sem, recv_sem, pass_sem, got_sem):
    me = lax.axis_index("expert")
    batch = lax.axis_index("dp")
    order = offsets_of(count)
    sources = (tok_ref, cot_ref)
    targets = (rows_ref, wrows_ref)

    def out_copy(a, o):
        peer = me ^ o
        return pltpu.make_async_remote_copy(
            src_ref=sources[a].at[peer],
            dst_ref=targets[a].at[batch, me],
            send_sem=send_sem.at[a, o],
            recv_sem=recv_sem.at[a, o],
            device_id=(peer, batch),
            device_id_type=MESH,
        )

    def in_copy(a, o):
        peer = me ^ o
        return pltpu.make_async_remote_copy(
            src_ref=sources[a].at[peer],
            dst_ref=targets[a].at[batch, peer],
            send_sem=send_sem.at[a, o],
            recv_sem=recv_sem.at[a, o],
            device_id=(peer, batch),
            device_id_type=MESH,
        )

    def pass_copy(a, o):
        peer = me ^ o
        src = targets[a].at[batch, peer] if o else sources[a].at[me]
        return pltpu.make_async_remote_copy(
            src_ref=src,
            dst_ref=targets[a].at[batch, peer],
            send_sem=pass_sem.at[a, o],
            recv_sem=got_sem.at[a, o],
            device_id=(me, 1 - batch),
            device_id_type=MESH,
        )

    def got_copy(a, o):
        peer = me ^ o
        return pltpu.make_async_remote_copy(
            src_ref=sources[a].at[peer],
            dst_ref=targets[a].at[1 - batch, peer],
            send_sem=pass_sem.at[a, o],
            recv_sem=got_sem.at[a, o],
            device_id=(me, 1 - batch),
            device_id_type=MESH,
        )

    def own_copy(a):
        return pltpu.make_async_copy(sources[a].at[me], targets[a].at[batch, me], local_sem.at[a])

    for o in order:
        out_copy(0, o).start()
    pass_copy(0, 0).start()
    own_copy(0).start()
    for o in order:
        in_copy(0, o).wait_recv()
        pass_copy(0, o).start()
        out_copy(1, o).start()
    pass_copy(1, 0).start()
    own_copy(1).start()
    for o in order:
        in_copy(1, o).wait_recv()
        pass_copy(1, o).start()
    for a in range(2):
        own_copy(a).wait()
        for o in order:
            out_copy(a, o).wait_send()
        for o in [0] + order:
            pass_copy(a, o).wait_send()
            got_copy(a, o).wait_recv()


def return_kernel(
    count, part_ref, dots_ref, back_ref, dback_ref, mine, got, total, load_sem, pass_sem, got_sem, send_sem, recv_sem, own_sem, dsend_sem, drecv_sem
):
    me = lax.axis_index("expert")
    batch = lax.axis_index("dp")
    order = offsets_of(count)

    def load_copy(o):
        peer = me ^ o
        return pltpu.make_async_copy(part_ref.at[batch, peer], mine.at[o], load_sem.at[o])

    def pass_copy(o):
        return pltpu.make_async_remote_copy(
            src_ref=part_ref.at[1 - batch, me ^ o],
            dst_ref=got.at[o],
            send_sem=pass_sem.at[o],
            recv_sem=got_sem.at[o],
            device_id=(me, 1 - batch),
            device_id_type=MESH,
        )

    def back_copy(o, slot):
        peer = me ^ o
        return pltpu.make_async_remote_copy(
            src_ref=total.at[o],
            dst_ref=back_ref.at[slot],
            send_sem=send_sem.at[o],
            recv_sem=recv_sem.at[o],
            device_id=(peer, batch),
            device_id_type=MESH,
        )

    def dot_copy(o, flip, slot_batch, slot):
        peer = me ^ o
        other = 1 - batch if flip else batch
        return pltpu.make_async_remote_copy(
            src_ref=dots_ref.at[other, peer],
            dst_ref=dback_ref.at[slot_batch, slot],
            send_sem=dsend_sem.at[flip, o],
            recv_sem=drecv_sem.at[flip, o],
            device_id=(peer, other),
            device_id_type=MESH,
        )

    def own_dots():
        return pltpu.make_async_copy(dots_ref.at[batch, me], dback_ref.at[batch, me], own_sem.at[1])

    def own_back():
        return pltpu.make_async_copy(total.at[0], back_ref.at[me], own_sem.at[0])

    for o in order + [0]:
        pass_copy(o).start()
        load_copy(o).start()
    own_dots().start()
    for o in [0] + order:
        for flip in range(2):
            if o or flip:
                dot_copy(o, flip, batch, me).start()
    for o in order + [0]:
        load_copy(o).wait()
        pass_copy(o).wait_recv()
        total[o] = (mine[o].astype(jnp.float32) + got[o].astype(jnp.float32)).astype(total.dtype)
        if o:
            back_copy(o, me).start()
        else:
            own_back().start()
    own_back().wait()
    own_dots().wait()
    for o in [0] + order:
        pass_copy(o).wait_send()
        if o:
            back_copy(o, me).wait_send()
            back_copy(o, me ^ o).wait_recv()
        for flip in range(2):
            if o or flip:
                dot_copy(o, flip, batch, me).wait_send()
                dot_copy(o, flip, 1 - batch if flip else batch, me ^ o).wait_recv()


def dispatch(tok_out, cot_out):
    count = tok_out.shape[0]
    shape = jax.ShapeDtypeStruct((2,) + tok_out.shape, tok_out.dtype)
    sems = pltpu.SemaphoreType.DMA((2, count))
    return pl.pallas_call(
        functools.partial(dispatch_kernel, count),
        out_shape=(shape, shape),
        in_specs=[ANY, ANY],
        out_specs=(ANY, ANY),
        scratch_shapes=[pltpu.SemaphoreType.DMA((2,)), sems, sems, sems, sems],
        compiler_params=pltpu.CompilerParams(has_side_effects=True, vmem_limit_bytes=4 * 2**20),
        name="dispatch",
    )(tok_out, cot_out)


def send_back(partial, dots):
    count = partial.shape[1]
    sems = pltpu.SemaphoreType.DMA((count,))
    pair_sems = pltpu.SemaphoreType.DMA((2, count))
    buffer = pltpu.VMEM(partial.shape[1:], partial.dtype)
    return pl.pallas_call(
        functools.partial(return_kernel, count),
        out_shape=(
            jax.ShapeDtypeStruct(partial.shape[1:], partial.dtype),
            jax.ShapeDtypeStruct(dots.shape, dots.dtype),
        ),
        in_specs=[ANY, ANY],
        out_specs=(ANY, ANY),
        scratch_shapes=[buffer, buffer, buffer, sems, sems, sems, sems, sems, pltpu.SemaphoreType.DMA((2,)), pair_sems, pair_sems],
        compiler_params=pltpu.CompilerParams(has_side_effects=True, vmem_limit_bytes=32 * 2**20),
        name="send_back",
    )(partial, dots)


def body(tokens, cotangent, expert_ids, slots, probs, w_gate, w_up, w_down):
    experts = lax.axis_size("expert")
    tok_rows, width = tokens.shape
    top_count = expert_ids.shape[1]
    capacity = max(2, 3 * tok_rows * top_count // (4 * experts))
    slot_total = experts * capacity
    kept = slots >= 0
    position = jnp.where(kept, expert_ids * capacity + slots, -1)
    slot_range = jnp.arange(slot_total, dtype=jnp.int32)
    hits = position.T[:, :, None] == slot_range[None, None, :]
    hot = jnp.any(hits, axis=0).astype(jnp.bfloat16)
    contract_first = (((0,), (0,)), ((), ()))
    slot_prob = jnp.sum(jnp.where(hits, probs.T[:, :, None], jnp.float32(0.0)), axis=(0, 1))
    tok_out = lax.dot_general(hot, tokens, contract_first, preferred_element_type=jnp.float32).astype(jnp.bfloat16)
    cot_out = (
        slot_prob[:, None] * lax.dot_general(hot, cotangent, contract_first, preferred_element_type=jnp.float32)
    ).astype(jnp.bfloat16)
    rows, wrows = dispatch(
        tok_out.reshape(experts, capacity, width), cot_out.reshape(experts, capacity, width)
    )
    pair_rows = rows.reshape(2 * slot_total, width)
    pair_cot = wrows.reshape(2 * slot_total, width)
    gate_w = w_gate[0]
    up_w = w_up[0]
    down_w = w_down[0]
    gate_pre = jnp.dot(pair_rows, gate_w, preferred_element_type=jnp.float32)
    up_pre = jnp.dot(pair_rows, up_w, preferred_element_type=jnp.float32)
    sigmoid_val = jax.nn.sigmoid(ALPHA * gate_pre)
    glu_value = gate_pre * sigmoid_val
    hidden = ((up_pre + 1.0) * glu_value).astype(jnp.bfloat16)
    contract_units = (((1,), (1,)), ((), ()))
    hidden_grad = jnp.dot(pair_cot, down_w, preferred_element_type=jnp.float32)
    dots = jnp.sum(hidden_grad * hidden.astype(jnp.float32), axis=1)
    up_grad = (hidden_grad * glu_value).astype(jnp.bfloat16)
    gate_grad = (
        hidden_grad
        * (up_pre + 1.0)
        * (sigmoid_val + ALPHA * gate_pre * sigmoid_val * (1.0 - sigmoid_val))
    ).astype(jnp.bfloat16)
    partial = (
        lax.dot_general(gate_grad, gate_w, contract_units, preferred_element_type=jnp.float32)
        + lax.dot_general(up_grad, up_w, contract_units, preferred_element_type=jnp.float32)
    ).astype(jnp.bfloat16)
    lanes = -(-capacity // 128) * 128
    dots = jnp.pad(dots.reshape(2, experts, 1, capacity), ((0, 0), (0, 0), (0, 0), (0, lanes - capacity)))
    back, dots_back = send_back(partial.reshape(2, experts, capacity, width), dots)
    grad_down = lax.dot_general(
        pair_cot, hidden, contract_first, preferred_element_type=jnp.float32
    ).astype(jnp.bfloat16)
    grad_gate = lax.dot_general(
        pair_rows, gate_grad, contract_first, preferred_element_type=jnp.float32
    ).astype(jnp.bfloat16)
    grad_up = lax.dot_general(
        pair_rows, up_grad, contract_first, preferred_element_type=jnp.float32
    ).astype(jnp.bfloat16)
    slot_dots = jnp.sum(dots_back[:, :, 0, :capacity], axis=0).reshape(slot_total)
    inner = jnp.sum(jnp.where(hits, slot_dots[None, None, :], jnp.float32(0.0)), axis=2).T
    prob_grad = jnp.where(kept, inner / probs, jnp.float32(0.0))
    input_grad = jnp.dot(
        hot, back.reshape(slot_total, width), preferred_element_type=jnp.float32
    ).astype(jnp.bfloat16)
    return (input_grad, prob_grad, grad_gate[None], grad_up[None], grad_down[None])


def solution(mesh):
    return jax.shard_map(
        body,
        mesh=mesh,
        in_specs=(
            P(("expert", "dp"), None),
            P(("expert", "dp"), None),
            P(("expert", "dp"), None),
            P(("expert", "dp"), None),
            P(("expert", "dp"), None),
            P("expert", None, "dp"),
            P("expert", None, "dp"),
            P("expert", None, "dp"),
        ),
        out_specs=(
            P(("expert", "dp"), None),
            P(("expert", "dp"), None),
            P("expert", None, "dp"),
            P("expert", None, "dp"),
            P("expert", None, "dp"),
        ),
        check_vma=False,
    )
```

time: 443 us -> 273 us (0.62)
  Pallas kernels: 0 us -> 202 us
  waiting for transfers between devices: 168 us -> 0 us
  blocking collectives: 113 us -> 0 us
  local copies, waits for them, and re-layouts: 52.4 us -> 18.2 us
  starting transfers between devices: 13.6 us -> 0 us
  between operations: 14.5 us -> 0.92 us
  matrix products: 60.4 us -> 47.7 us
  other arithmetic: 14.1 us -> 2.01 us
    pallas_call x0 -> x2, Pallas kernels: none -> 202 us  [the longest x1 140 us: dispatch(): pl.pallas_call(functools.partial(dispatch_kernel, count), out_shape=(shap...]
    all_to_all x2 -> x0, blocking collectives: 113 us -> none  [the longest x1 57.2 us: body(): lax.all_to_all(outgoing.reshape(experts, capacity, width), 'expert', spli...]
    reduce_scatter x2 -> x0, waiting for transfers between devices: 95.9 us -> none  [the longest x1 53.6 us: body(): lax.psum_scatter(lax.dot_general(hidden, down_w, contract_units, preferre...]
    all_gather x2 -> x0, waiting for transfers between devices: 58.9 us -> none  [the longest x1 55.2 us: body(): pair_cot = lax.all_gather(weighted, 'dp', axis=0, tiled=True)]
    gather x6 -> x0, local copies, waits for them, and re-layouts: 25.7 us -> none  [the longest x2 10.4 us: body(): picked_out = returned.reshape(slot_total, width)[lookup]]
    unnamed x35 -> x40, local copies, waits for them, and re-layouts: 20.8 us -> 4.19 us
    convert_element_type x0 -> x3, local copies, waits for them, and re-layouts: none -> 13.8 us  [the longest x1 6.61 us: body(): partial = (lax.dot_general(gate_grad, gate_w, contract_units, preferred_e...]
    all_to_all x2 -> x0, waiting for transfers between devices: 13.2 us -> none  [the longest x1 13.2 us: body(): lax.all_to_all(own_out.reshape(experts, capacity, width), 'expert', split...]
  transfers between devices with their start and end apart: 6 -> 0, of which waited for: 5 -> 0; matrix products, arithmetic and copies ran while one was open for 14% -> 0% of each run, Pallas kernels for 0% -> 0%
where the time goes in v1:
time: 273 us; the launch traced here: 271 us
  Pallas kernels  202 us (74%)
  matrix products  47.7 us (17%)
  local copies, waits for them, and re-layouts  18.2 us (7%)
    pallas_call x1, Pallas kernels, dispatch(): pl.pallas_call(functools.partial(dispatch_kernel, count), out_shape=(shap...  140 us
    pallas_call x1, Pallas kernels, send_back(): pl.pallas_call(functools.partial(return_kernel, count), out_shape=(jax.Sh...  61.5 us
    dot_general x1, matrix products, body(): lax.dot_general(pair_rows, gate_grad, contract_first, preferred_element_t...  8.38 us
    convert_element_type x1, local copies, waits for them, and re-layouts, body(): partial = (lax.dot_general(gate_grad, gate_w, contract_units, preferred_e...  6.61 us
    dot_general x1, matrix products, body(): lax.dot_general(up_grad, up_w, contract_units, preferred_element_type=jnp...  6.14 us
    dot_general x1, matrix products, body(): hidden_grad = jnp.dot(pair_cot, down_w, preferred_element_type=jnp.float32)  5.6 us

profile of v1, /device:TPU:13, one launch (start us, length us, event | category | flops | bytes accessed | tf_op | source)
XLA Modules:
  0.0 270.6 jit_solution(12666418621495007192)
XLA Ops:
  0.7 0.8 select_bitcast_fusion
  1.4 0.2 fusion.14
  1.6 0.2 copy-done
  1.8 2.1 convolution_convert_fusion.3
  3.9 3.0 %copy.16 = bf16[384,2880]{1,0:T(8,128)(2,1)S(1)} copy(bf16[384,2880]{0,1:T(8,128)(2,1)} %convolution_convert_fusion.3) | data formatting | bytes 4423680 | tf_op jit(solution)/shard_map/convert_element_type | solution.py:228
  6.9 0.2 select_reduce_fusion.1
  7.1 2.1 fusion.12
  9.2 4.2 %copy.17 = bf16[384,2880]{1,0:T(8,128)(2,1)} copy(bf16[384,2880]{0,1:T(8,128)(2,1)} %fusion.12) | data formatting | bytes 4423680 | tf_op jit(solution)/shard_map/convert_element_type | solution.py:231
  13.4 1.6 copy-done.3
  15.0 140.2 %dispatch.1 = (bf16[2,16,24,2880]{3,2,1,0:T(8,128)(2,1)S(1)}, bf16[2,16,24,2880]{3,2,1,0:T(8,128)(2,1)S(1)}) custom-call(bf16[16,24,2880]{2,1,0:T(8,128)(2,1)S(1)} %bitcast.52, bf16[16,24,2880]{2,1,0:T(8,128)(2,1)S(1)} %bitcast.53), custom_call_target="tpu_custom_call" | custom-call | tf_op jit(solution)/shard_map/dispatch/pallas_call | solution.py:185
  155.3 3.6 %fusion.5 = f32[768,720]{0,1:T(8,128)S(1)} fusion(bf16[768,2880]{1,0:T(8,128)(2,1)S(1)} %bitcast.59, bf16[1,2880,720]{1,2,0:T(8,128)(2,1)S(1)} %copy-done.9), kind=kOutput, calls=%fused_computation.10 | convolution fusion | flops 3185049600 | bytes 10782720 | tf_op jit(solution)/shard_map/dot_general | solution.py:240
  159.0 3.6 %fusion.8 = f32[768,720]{0,1:T(8,128)S(1)} fusion(bf16[768,2880]{1,0:T(8,128)(2,1)S(1)} %bitcast.60, bf16[1,2880,720]{1,2,0:T(8,128)(2,1)S(1)} %bitcast.69), kind=kOutput, calls=%fused_computation.13 | convolution fusion | flops 3185049600 | bytes 10782720 | tf_op jit(solution)/shard_map/dot_general | solution.py:241
  162.7 5.6 %multiply_reduce_fusion = (f32[768]{0:T(1024)S(1)}, bf16[768,720]{0,1:T(8,128)(2,1)}, bf16[768,720]{0,1:T(8,128)(2,1)S(1)}, bf16[768,720]{0,1:T(8,128)(2,1)S(1)}) fusion(f32[768,720]{0,1:T(8,128)S(1)} %fusion.5, f32[768,720]{0,1:T(8,128)S(1)} %fusion.8, bf16[768,2880]{1,0:T(8,128)(2,1)S(1)} %bitcast.55, bf16[1,2880,720]{1,2,0:T(8,128)(2,1)S(1)} %bitcast.67), kind=kOutput, calls=%fused_computation.20 | convolution fusion | flops 3196108032 | bytes 16315392 | tf_op jit(solution)/shard_map/dot_general | solution.py:246
  168.3 4.0 %fusion.3 = f32[768,2880]{0,1:T(8,128)S(1)} fusion(bf16[768,720]{0,1:T(8,128)(2,1)S(1)} %get-tuple-element.15, bf16[1,2880,720]{1,2,0:T(8,128)(2,1)S(1)} %copy-done.9), kind=kOutput, calls=%fused_computation.8 | convolution fusion | flops 3185049600 | bytes 14100480 | tf_op jit(solution)/shard_map/dot_general | solution.py:255
  172.3 6.1 %add_convert_fusion = bf16[768,2880]{0,1:T(8,128)(2,1)} fusion(f32[768,2880]{0,1:T(8,128)S(1)} %fusion.3, bf16[768,720]{0,1:T(8,128)(2,1)S(1)} %get-tuple-element.16, bf16[1,2880,720]{1,2,0:T(8,128)(2,1)S(1)} %bitcast.69), kind=kOutput, calls=%fused_computation | convolution fusion | flops 3189473280 | bytes 18524160 | tf_op jit(solution)/shard_map/dot_general | solution.py:256
  178.4 6.6 %copy.18 = bf16[768,2880]{1,0:T(8,128)(2,1)} copy(bf16[768,2880]{0,1:T(8,128)(2,1)} %add_convert_fusion) | data formatting | bytes 8847360 | tf_op jit(solution)/shard_map/convert_element_type | solution.py:257
  185.2 2.3 copy-done.2
  187.5 61.5 %send_back.1 = (bf16[16,24,2880]{2,1,0:T(8,128)(2,1)S(1)}, f32[2,16,1,128]{3,2,1,0:T(1,128)S(1)}) custom-call(bf16[2,16,24,2880]{3,2,1,0:T(8,128)(2,1)S(1)} %bitcast.51, f32[2,16,1,128]{3,2,1,0:T(1,128)S(1)} %pad.4.dots_ref), custom_call_target="tpu_custom_call" | custom-call | tf_op jit(solution)/shard_map/send_back/pallas_call | solution.py:201
  249.0 1.9 convolution_convert_fusion.4
  251.0 0.3 select_reduce_fusion
  251.3 0.6 fusion.15
  251.9 8.4 %fusion = bf16[1,2880,720]{1,2,0:T(8,128)(2,1)} fusion(bf16[768,720]{0,1:T(8,128)(2,1)} %copy-done.10, bf16[768,2880]{1,0:T(8,128)(2,1)} %bitcast.61), kind=kOutput, calls=%fused_computation.5 | convolution fusion | flops 3187123200 | bytes 9676800 | tf_op jit(solution)/shard_map/dot_general | solution.py:264
  260.3 5.1 %fusion.1 = bf16[1,2880,720]{1,2,0:T(8,128)(2,1)} fusion(bf16[768,720]{0,1:T(8,128)(2,1)S(1)} %get-tuple-element.16, bf16[768,2880]{1,0:T(8,128)(2,1)S(1)} %bitcast.64), kind=kOutput, calls=%fused_computation.6 | convolution fusion | flops 3187123200 | bytes 9676800 | tf_op jit(solution)/shard_map/dot_general | solution.py:267
  265.4 5.2 %fusion.2 = bf16[1,2880,720]{1,2,0:T(8,128)(2,1)} fusion(bf16[768,720]{0,1:T(8,128)(2,1)S(1)} %copy-done.11, bf16[768,2880]{1,0:T(8,128)(2,1)S(1)} %bitcast.58), kind=kOutput, calls=%fused_computation.7 | convolution fusion | flops 3187123200 | bytes 9676800 | tf_op jit(solution)/shard_map/dot_general | solution.py:261
  (45 shorter events, 0.3 us)
Async XLA Ops:
  0.6 1.2 copy-start
  0.6 6.2 %copy-start.8 = (f32[128,4]{0,1:T(4,128)S(1)}, f32[128,4]{0,1:T(4,128)}, u32[]{:S(2)}) copy-start(f32[128,4]{0,1:T(4,128)} %param.12) | copy-start | bytes 6148
  3.9 3.2 %copy-start.6 = (bf16[128,2880]{0,1:T(8,128)(2,1)S(1)}, bf16[128,2880]{0,1:T(8,128)(2,1)}, u32[]{:S(2)}) copy-start(bf16[128,2880]{0,1:T(8,128)(2,1)} %param.9) | copy-start | bytes 2211844
  13.4 1.6 copy-start.3
  15.0 140.3 %copy-start.9 = (bf16[1,2880,720]{1,2,0:T(8,128)(2,1)S(1)}, bf16[1,2880,720]{1,2,0:T(8,128)(2,1)}, u32[]{:S(2)}) copy-start(bf16[1,2880,720]{1,2,0:T(8,128)(2,1)} %param.13) | copy-start | bytes 12441604
  15.0 144.0 %slice-start.6 = ((s8[4239360]{0:T(1024)(128)(4,1)}), s8[4194304]{0:T(1024)(128)(4,1)S(1)}, s32[]{:S(2)}) async-start(s8[4239360]{0:T(1024)(128)(4,1)} %bitcast.68), calls=%async_computation.6 | async-start | bytes 8388608
  155.3 3.7 %copy-start.5 = (bf16[2,16,24,2880]{3,2,1,0:T(8,128)(2,1)}, bf16[2,16,24,2880]{3,2,1,0:T(8,128)(2,1)S(1)}, u32[]{:S(2)}) copy-start(bf16[2,16,24,2880]{3,2,1,0:T(8,128)(2,1)S(1)} %get-tuple-element.10) | copy-start | bytes 13271044
  155.3 7.4 %copy-start.4 = (bf16[2,16,24,2880]{3,2,1,0:T(8,128)(2,1)}, bf16[2,16,24,2880]{3,2,1,0:T(8,128)(2,1)S(1)}, u32[]{:S(2)}) copy-start(bf16[2,16,24,2880]{3,2,1,0:T(8,128)(2,1)S(1)} %get-tuple-element.9) | copy-start | bytes 13271044
  155.3 3.7 %slice-start.7 = ((s8[4239360]{0:T(1024)(128)(4,1)}), s8[45056]{0:T(1024)(128)(4,1)S(1)}, s32[]{:S(2)}) async-start(s8[4239360]{0:T(1024)(128)(4,1)} %bitcast.68), calls=%async_computation.7 | async-start | bytes 90112
  155.3 7.3 %slice-start.4 = ((s8[4239360]{0:T(1024)(128)(4,1)}), s8[4194304]{0:T(1024)(128)(4,1)S(1)}, s32[]{:S(2)}) async-start(s8[4239360]{0:T(1024)(128)(4,1)} %bitcast.66), calls=%async_computation.4 | async-start | bytes 8388608
  159.0 3.7 %slice-start.5 = ((s8[4239360]{0:T(1024)(128)(4,1)}), s8[45056]{0:T(1024)(128)(4,1)S(1)}, s32[]{:S(2)}) async-start(s8[4239360]{0:T(1024)(128)(4,1)} %bitcast.66), calls=%async_computation.5 | async-start | bytes 90112
  168.3 4.0 %copy-start.10 = (bf16[768,720]{0,1:T(8,128)(2,1)}, bf16[768,720]{0,1:T(8,128)(2,1)S(1)}, u32[]{:S(2)}) copy-start(bf16[768,720]{0,1:T(8,128)(2,1)S(1)} %get-tuple-element.15) | copy-start | bytes 3317764
  185.1 66.2 %copy-start.7 = (s32[128,4]{0,1:T(4,128)S(1)}, s32[128,4]{0,1:T(4,128)}, u32[]{:S(2)}) copy-start(s32[128,4]{0,1:T(4,128)} %param.11) | copy-start | bytes 6148
  185.2 2.3 copy-start.2
  249.0 11.3 %slice-start.2 = ((s8[4521984]{0:T(1024)(128)(4,1)}), s8[327680]{0:T(1024)(128)(4,1)S(1)}, s32[]{:S(2)}) async-start(s8[4521984]{0:T(1024)(128)(4,1)} %bitcast.62), calls=%async_computation.2 | async-start | bytes 655360
  251.9 8.4 %slice-start.3 = ((s8[4521984]{0:T(1024)(128)(4,1)}), s8[4194304]{0:T(1024)(128)(4,1)S(1)}, s32[]{:S(2)}) async-start(s8[4521984]{0:T(1024)(128)(4,1)} %bitcast.62), calls=%async_computation.3 | async-start | bytes 8388608
  251.9 13.5 %slice-start = ((s8[4521984]{0:T(1024)(128)(4,1)}), s8[4194304]{0:T(1024)(128)(4,1)S(1)}, s32[]{:S(2)}) async-start(s8[4521984]{0:T(1024)(128)(4,1)} %bitcast.56), calls=%async_computation | async-start | bytes 8388608
  260.3 5.1 %slice-start.1 = ((s8[4521984]{0:T(1024)(128)(4,1)}), s8[327680]{0:T(1024)(128)(4,1)S(1)}, s32[]{:S(2)}) async-start(s8[4521984]{0:T(1024)(128)(4,1)} %bitcast.56), calls=%async_computation.1 | async-start | bytes 655360
  260.3 5.1 %copy-start.11 = (bf16[768,720]{0,1:T(8,128)(2,1)S(1)}, bf16[768,720]{0,1:T(8,128)(2,1)}, u32[]{:S(2)}) copy-start(bf16[768,720]{0,1:T(8,128)(2,1)} %get-tuple-element.14) | copy-start | bytes 3317764
  265.4 5.2 %copy-start.1 = (bf16[128,2880]{0,1:T(8,128)(2,1)S(1)}, bf16[128,2880]{0,1:T(8,128)(2,1)}, u32[]{:S(2)}) copy-start(bf16[128,2880]{0,1:T(8,128)(2,1)} %param.8) | copy-start | bytes 2211844
